TPU v7x, 32 devices: a whole 2x2x4 slice. The times are simulated.
32 devices in a mesh: node: 32 (over z, y, x, core).
Axes of the slice: x: 2, y: 2, z: 4, core: 2. Of those that a mesh axis runs over, the one named last changes fastest.
Arguments:
- labels: bfloat16 [131072, 512], P('node'), may hold values from -6 to 6
- seed_mask: int32 [131072], P('node'), may hold values 0 or 1
- band_w: bfloat16 [1024, 3, 128, 128], P('node'), may hold values from 0.0009994507 to 1
- far_block: int32 [32, 32, 2], P('node'), may hold values from 0 to 511
- far_tile: int32 [32, 32, 2], P('node'), may hold values from 0 to 31
- far_count: int32 [32, 32], P('node'), may hold values from 0 to 2, as said below
- far_w: bfloat16 [32, 32, 2, 8, 128], P('node'), may hold values from 0.049804688 to 2
Outputs:
- final_labels: bfloat16 [131072, 512], P('node')
- residual: float32 [2, 1024], P(None, 'node')
Inputs may be any that keep to these rules, and one draw needn't show every extreme that they name: `far_count`: in every draw at least one destination shard has all 2 slots live from every source shard; other counts vary from pair to pair.
All inputs are finite; a program needn't handle non-finite values. No bound on the sum of `seed_mask` on one device may be relied on, other than what follows from the above.
Results may differ from a plain program's by a relative error of at most 0.0027.
Values may be sent and summed in bfloat16 or wider, within the bound.
A program may use at most 128 MiB of HBM per device.

v0:
```python
import jax
import jax.numpy as jnp
from jax import lax
from jax.sharding import PartitionSpec as P

ITERS = 2


def with_halo(block, sides, width):
    for axis, dim in sides:
        count = lax.axis_size(axis)
        forward = [(i, i + 1) for i in range(count - 1)]
        forward.append((count - 1, 0))
        backward = [(target, source) for source, target in forward]
        low = lax.ppermute(
            lax.slice_in_dim(block, block.shape[dim] - width, None, axis=dim), axis, forward
        )
        high = lax.ppermute(lax.slice_in_dim(block, 0, width, axis=dim), axis, backward)
        block = jnp.concatenate([low, block, high], axis=dim)
    return block


def fetch_blocks(current, requests, block_rows, classes):
    blocks = current.reshape(-1, block_rows, classes)[requests]
    return lax.all_to_all(blocks, "node", split_axis=0, concat_axis=0, tiled=True)


def cycle_tiles(current, tile_count, tile_rows, classes):
    tiles = current.reshape(tile_count, tile_rows, classes)
    return with_halo(tiles, (("node", 0),), 1)


def body(labels, seed_mask, band_w, far_block, far_tile, far_count, far_w):
    node_rows, classes = labels.shape
    tile_count = band_w.shape[0]
    tile_rows = band_w.shape[2]
    peer_count = far_w.shape[1]
    slot_count = far_w.shape[2]
    block_rows = far_w.shape[3]
    requests = lax.all_to_all(far_block, "node", split_axis=1, concat_axis=0, tiled=True).reshape(
        peer_count, slot_count
    )
    live_slots = jnp.arange(slot_count)[None, :] < far_count[0][:, None]
    weights = jnp.where(live_slots[:, :, None, None], far_w[0], jnp.zeros((), jnp.bfloat16))
    flat_tiles = far_tile[0].reshape(-1)
    weight_sums = jnp.sum(weights, axis=2, dtype=jnp.float32).reshape(-1, tile_rows)
    degree_far = jnp.zeros((tile_count, tile_rows), jnp.float32).at[flat_tiles].add(weight_sums)
    degree = jnp.sum(band_w, axis=(1, 3), dtype=jnp.float32) + degree_far
    slot_weights = weights.reshape(peer_count * slot_count, block_rows, tile_rows)
    onehot = jnp.arange(tile_count)[:, None] == flat_tiles[None, :]
    placed = jnp.where(onehot[:, :, None, None], slot_weights[None], jnp.zeros((), jnp.bfloat16))
    placed = placed.reshape(tile_count, peer_count * slot_count * block_rows, tile_rows)
    seeded = (seed_mask == 1).reshape(tile_count, tile_rows, 1)
    clamped = labels.astype(jnp.float32).reshape(tile_count, tile_rows, classes)
    current = labels
    residuals = []
    for sweep in range(ITERS):
        padded = cycle_tiles(current, tile_count, tile_rows, classes)
        received = fetch_blocks(current, requests, block_rows, classes)
        band_sum = jnp.zeros((tile_count, tile_rows, classes), jnp.float32)
        for offset in (-1, 0, 1):
            source = padded[1 + offset : 1 + offset + tile_count]
            band_sum = band_sum + jnp.einsum(
                "itr,irc->itc", band_w[:, offset + 1], source, preferred_element_type=jnp.float32
            )
        far_sum = jnp.einsum(
            "tqr,qc->trc", placed, received.reshape(-1, classes), preferred_element_type=jnp.float32
        )
        averaged = (band_sum + far_sum) / degree[:, :, None]
        row_scale = jnp.sqrt(jnp.mean(averaged * averaged, axis=2, keepdims=True))
        scaled = averaged / jnp.maximum(row_scale, 0.05)
        fresh = jnp.where(seeded, clamped, scaled).astype(jnp.bfloat16)
        previous = current.astype(jnp.float32).reshape(tile_count, tile_rows, classes)
        residuals.append(jnp.sum(jnp.abs(fresh.astype(jnp.float32) - previous), axis=(1, 2)))
        current = fresh.reshape(node_rows, classes)
    return (current, jnp.stack(residuals))


def solution(mesh):
    placed = (
        P("node", None),
        P("node"),
        P("node", None, None, None),
        P("node", None, None),
        P("node", None, None),
        P("node", None),
        P("node", None, None, None, None),
    )
    return jax.shard_map(
        body,
        mesh=mesh,
        in_specs=placed,
        out_specs=(P("node", None), P(None, "node")),
        check_vma=False,
    )
```

profile of v0, /device:TPU:0, one launch (start us, length us, event | category | flops | bytes accessed | tf_op | source)
XLA Modules:
  0.0 134.0 jit_solution(6983224722722546354)
XLA Ops:
  0.7 1.5 %copy.30 = s32[1,32,2]{2,0,1:T(1,128)} copy(s32[1,32,2]{1,2,0:T(2,128)} %param.10) | data formatting | bytes 512 | tf_op args[3]
  2.2 7.5 %all-to-all-start = ((s32[1,32,2]{2,0,1:T(1,128)}), s32[1,32,2]{2,0,1:T(1,128)}, u32[]{:S(2)}, u32[]{:S(2)}) async-start(s32[1,32,2]{2,0,1:T(1,128)} %copy.30), calls=%async_computation | async-start | bytes 32768 | tf_op jit(solution)/shard_map/all_to_all | solution.py:40
  9.6 1.7 %slice_bitcast_fusion = (bf16[1,128,512]{2,1,0:T(8,128)(2,1)}, bf16[1,128,512]{2,1,0:T(8,128)(2,1)}) fusion(bf16[4096,512]{1,0:T(8,128)(2,1)} %param.7), kind=kLoop, calls=%fused_computation.59 | loop fusion | bytes 524288 | tf_op jit(solution)/shard_map/slice | solution.py:18
  11.4 5.1 %collective-permute-start.1 = (bf16[1,128,512]{2,1,0:T(8,128)(2,1)}, bf16[1,128,512]{2,1,0:T(8,128)(2,1)}, u32[]{:S(2)}, u32[]{:S(2)}) collective-permute-start(bf16[1,128,512]{2,1,0:T(8,128)(2,1)} %get-tuple-element.6), channel_id=1, source_target_pairs={{1,0},{2,1},{3,2},{4,3},{5,4},{6,5},{7,6},{8,7},{9,8},{10,9},{11,1... | collective-permute-start | bytes 393224 | tf_op jit(solution)/shard_map/ppermute | solution.py:18
  16.5 0.8 copy.27
  17.5 0.7 iota_compare_fusion.1
  18.5 0.5 fusion.39
  19.1 2.5 %convert_reduce_fusion = f32[32,128]{1,0:T(8,128)S(1)} fusion(bf16[32,3,128,128]{3,2,1,0:T(8,128)(2,1)} %param.9), kind=kLoop, calls=%fused_computation.19 | loop fusion | flops 3141632 | bytes 3162112 | tf_op jit(solution)/shard_map/reduce_sum | solution.py:48
  21.6 1.0 bitcast_select_fusion.1
  22.7 0.8 convert_reduce_fusion.1
  23.7 1.1 scatter_fusion
  24.9 0.8 copy.31
  25.9 3.6 %gather_fusion = bf16[64,8,512]{2,1,0:T(8,128)(2,1)} fusion(bf16[512,8,512]{2,1,0:T(8,128)(2,1)} %bitcast.77, s32[1024]{0:T(1024)S(1)} %pad_clamp_fusion), kind=kCustom, calls=%fused_computation | custom fusion | bytes 1048832 | tf_op jit(solution)/shard_map/gather | solution.py:24
  29.5 5.8 %all-to-all-start.1 = ((bf16[32,2,8,512]{3,2,1,0:T(8,128)(2,1)}), bf16[32,2,8,512]{3,2,1,0:T(8,128)(2,1)}, u32[]{:S(2)}, u32[]{:S(2)}) async-start(bf16[32,2,8,512]{3,2,1,0:T(8,128)(2,1)} %bitcast.85), calls=%async_computation.1 | async-start | bytes 1048576 | tf_op jit(solution)/shard_map/all_to_all | solution.py:25
  35.4 6.8 %fusion.29 = f32[32,128,512]{2,1,0:T(8,128)} fusion(bf16[32,128,512]{2,1,0:T(8,128)(2,1)} %bitcast.78, bf16[32,3,128,128]{3,2,1,0:T(8,128)(2,1)S(1)} %copy-done.6), kind=kOutput, calls=%fused_computation.46 | convolution fusion | flops 536870912 | bytes 13631488 | tf_op jit(solution)/shard_map/itr,irc->itc/dot_general | solution.py:63
  42.2 5.4 %fusion.17 = f32[32,512,128]{1,2,0:T(8,128)} fusion(bf16[32,128,512]{2,1,0:T(8,128)(2,1)S(1)} %bitcast.79, bf16[1,128,512]{2,1,0:T(8,128)(2,1)} %collective-permute-done, bf16[32,3,128,128]{3,2,1,0:T(8,128)(2,1)S(1)} %copy-done.6), kind=kOutput, calls=%fused_computation.34 | convolution fusion | flops 545259520 | bytes 13762560 | tf_op jit(solution)/shard_map/itr,irc->itc/dot_general | solution.py:63
  47.6 3.3 %all-to-all-done.1 = bf16[32,2,8,512]{3,2,1,0:T(8,128)(2,1)} async-done(((bf16[32,2,8,512]{3,2,1,0:T(8,128)(2,1)}), bf16[32,2,8,512]{3,2,1,0:T(8,128)(2,1)}, u32[]{:S(2)}, u32[]{:S(2)}) %all-to-all-start.1) | async-done | bytes 524320 | tf_op jit(solution)/shard_map/all_to_all | solution.py:25
  50.9 6.8 %fusion.9 = f32[32,128,512]{2,1,0:T(8,128)} fusion(bf16[512,512,1]{1,0,2:T(8,128)(2,1)} %bitcast.16, pred[32,512]{1,0:T(8,128)(4,1)S(1)} %copy.28, bf16[512,128]{0,1:T(8,128)(2,1)S(1)} %copy.29), kind=kOutput, calls=%fused_computation.22 | convolution fusion | flops 2149580800 | bytes 9060352 | tf_op jit(solution)/shard_map/tqr,qc->trc/dot_general | solution.py:66
  57.7 13.6 %multiply_reduce_fusion.1 = (f32[32,128]{1,0:T(8,128)S(1)}, f32[32,128,512]{2,1,0:T(8,128)}) fusion(f32[32,128]{1,0:T(8,128)S(1)} %scatter_fusion, f32[32,128,512]{2,1,0:T(8,128)} %fusion.9, bf16[1,128,512]{2,1,0:T(8,128)(2,1)} %collective-permute-done.1, bf16[32,128,512]{2,1,0:T(8,128)(2,1)S(1)} %bitcast.80, bf16[32,3,128,128]{3,2,1,0:T(8,128)(2,1)S(1)} %copy-done.6, ...), kind=kOutput, calls=%fused_computation.18 | convolution fusion | flops 557838336 | bytes 38961152 | tf_op jit(solution)/shard_map/itr,irc->itc/dot_general | solution.py:63
  71.3 5.0 %fusion.2 = bf16[32,128,512]{2,1,0:T(8,128)(2,1)S(1)} fusion(f32[32,128,512]{2,1,0:T(8,128)} %get-tuple-element.9, f32[32,128]{1,0:T(8,128)S(1)} %maximum_multiply_fusion.1, pred[32,128]{1,0:T(8,128)(4,1)S(1)} %compare_bitcast_fusion, bf16[4096,512]{1,0:T(8,128)(2,1)S(1)} %copy-done.1), kind=kLoop, calls=%fused_computation.9 | loop fusion | flops 8388608 | bytes 16797696 | tf_op jit(solution)/shard_map/convert_element_type | solution.py:72
  76.3 2.0 %copy-done.3 = bf16[32,128,512]{2,1,0:T(8,128)(2,1)} copy-done((bf16[32,128,512]{2,1,0:T(8,128)(2,1)}, bf16[32,128,512]{2,1,0:T(8,128)(2,1)S(1)}, u32[]{:S(2)}) %copy-start.3) | copy-done | bytes 4194328
  78.3 0.7 fusion.46
  79.0 3.6 %gather_fusion.1 = bf16[64,8,512]{2,1,0:T(8,128)(2,1)} fusion(bf16[512,8,512]{2,1,0:T(8,128)(2,1)} %bitcast.82, s32[1024]{0:T(1024)S(1)} %pad_clamp_fusion), kind=kCustom, calls=%fused_computation.1 | custom fusion | bytes 1048832 | tf_op jit(solution)/shard_map/gather | solution.py:24
  82.6 5.8 %all-to-all-start.2 = ((bf16[32,2,8,512]{3,2,1,0:T(8,128)(2,1)}), bf16[32,2,8,512]{3,2,1,0:T(8,128)(2,1)}, u32[]{:S(2)}, u32[]{:S(2)}) async-start(bf16[32,2,8,512]{3,2,1,0:T(8,128)(2,1)} %bitcast.84), calls=%async_computation.2 | async-start | bytes 1048576 | tf_op jit(solution)/shard_map/all_to_all | solution.py:25
  88.4 6.8 %fusion.27 = f32[32,512,128]{1,2,0:T(8,128)} fusion(bf16[32,128,512]{2,1,0:T(8,128)(2,1)} %copy-done.3, bf16[32,3,128,128]{3,2,1,0:T(8,128)(2,1)S(1)} %copy-done.6), kind=kOutput, calls=%fused_computation.44 | convolution fusion | flops 536870912 | bytes 13631488 | tf_op jit(solution)/shard_map/itr,irc->itc/dot_general | solution.py:63
  95.2 5.1 %collective-permute-start.3 = (bf16[1,128,512]{2,1,0:T(8,128)(2,1)}, bf16[1,128,512]{2,1,0:T(8,128)(2,1)}, u32[]{:S(2)}, u32[]{:S(2)}) collective-permute-start(bf16[1,128,512]{2,1,0:T(8,128)(2,1)} %get-tuple-element.4), channel_id=1, source_target_pairs={{1,0},{2,1},{3,2},{4,3},{5,4},{6,5},{7,6},{8,7},{9,8},{10,9},{11,1... | collective-permute-start | bytes 393224 | tf_op jit(solution)/shard_map/ppermute | solution.py:18
  100.4 4.5 %fusion.13 = f32[32,512,128]{1,2,0:T(8,128)} fusion(bf16[32,128,512]{2,1,0:T(8,128)(2,1)S(1)} %copy-done.4, bf16[1,128,512]{2,1,0:T(8,128)(2,1)S(1)} %collective-permute-done.2, bf16[32,3,128,128]{3,2,1,0:T(8,128)(2,1)S(1)} %copy-done.6), kind=kOutput, calls=%fused_computation.28 | convolution fusion | flops 545259520 | bytes 13762560 | tf_op jit(solution)/shard_map/itr,irc->itc/dot_general | solution.py:63
  104.8 6.8 %fusion.7 = f32[32,128,512]{2,1,0:T(8,128)} fusion(bf16[512,512,1]{1,0,2:T(8,128)(2,1)} %bitcast.24, pred[32,512]{1,0:T(8,128)(4,1)S(1)} %copy-done.10, bf16[512,128]{0,1:T(8,128)(2,1)S(1)} %copy.29), kind=kOutput, calls=%fused_computation.20 | convolution fusion | flops 2149580800 | bytes 9060352 | tf_op jit(solution)/shard_map/tqr,qc->trc/dot_general | solution.py:66
  111.6 13.7 %multiply_reduce_fusion = (f32[32,128]{1,0:T(8,128)S(1)}, f32[32,128,512]{2,1,0:T(8,128)}) fusion(f32[32,128]{1,0:T(8,128)S(1)} %scatter_fusion, f32[32,128,512]{2,1,0:T(8,128)} %fusion.7, bf16[1,128,512]{2,1,0:T(8,128)(2,1)} %collective-permute-done.3, bf16[32,128,512]{2,1,0:T(8,128)(2,1)S(1)} %copy-done.5, bf16[32,3,128,128]{3,2,1,0:T(8,128)(2,1)} %param.9, ...), kind=kOutput, calls=%fused_computation.17 | convolution fusion | flops 557838336 | bytes 38961152 | tf_op jit(solution)/shard_map/itr,irc->itc/dot_general | solution.py:63
  125.4 5.0 %fusion.3 = bf16[32,128,512]{2,1,0:T(8,128)(2,1)S(1)} fusion(f32[32,128,512]{2,1,0:T(8,128)} %get-tuple-element.11, f32[32,128]{1,0:T(8,128)S(1)} %maximum_multiply_fusion, pred[32,128]{1,0:T(8,128)(4,1)S(1)} %compare_bitcast_fusion, bf16[4096,512]{1,0:T(8,128)(2,1)S(1)} %copy-done.2), kind=kLoop, calls=%fused_computation.10 | loop fusion | flops 8388608 | bytes 16797696 | tf_op jit(solution)/shard_map/convert_element_type | solution.py:72
  130.4 3.1 %fusion.5 = (f32[32]{0:T(128)S(1)}, f32[32]{0:T(128)S(1)}) fusion(bf16[32,128,512]{2,1,0:T(8,128)(2,1)S(1)} %bitcast.81, bf16[32,128,512]{2,1,0:T(8,128)(2,1)S(1)} %copy-done.5, bf16[32,128,512]{2,1,0:T(8,128)(2,1)S(1)} %fusion.3), kind=kLoop, calls=%fused_computation.12 | loop fusion | flops 18874304 | bytes 12583168 | tf_op jit(solution)/shard_map/reduce_sum | solution.py:74
  133.4 0.6 pad_maximum_fusion.12
  (47 shorter events, 1.2 us)
Async XLA Ops:
  0.6 34.7 %copy-start.6 = (bf16[32,3,128,128]{3,2,1,0:T(8,128)(2,1)S(1)}, bf16[32,3,128,128]{3,2,1,0:T(8,128)(2,1)}, u32[]{:S(2)}) copy-start(bf16[32,3,128,128]{3,2,1,0:T(8,128)(2,1)} %param.9) | copy-start | bytes 9437188
  0.6 22.0 %copy-start.8 = (bf16[1,32,2,8,128]{4,3,2,1,0:T(8,128)(2,1)S(1)}, bf16[1,32,2,8,128]{4,3,2,1,0:T(8,128)(2,1)}, u32[]{:S(2)}) copy-start(bf16[1,32,2,8,128]{4,3,2,1,0:T(8,128)(2,1)} %param.13) | copy-start | bytes 393220
  2.2 22.7 %all-to-all-start = ((s32[1,32,2]{2,0,1:T(1,128)}), s32[1,32,2]{2,0,1:T(1,128)}, u32[]{:S(2)}, u32[]{:S(2)}) async-start(s32[1,32,2]{2,0,1:T(1,128)} %copy.30), calls=%async_computation | async-start | bytes 32768 | tf_op jit(solution)/shard_map/all_to_all | solution.py:40
  11.4 46.3 %collective-permute-start.1 = (bf16[1,128,512]{2,1,0:T(8,128)(2,1)}, bf16[1,128,512]{2,1,0:T(8,128)(2,1)}, u32[]{:S(2)}, u32[]{:S(2)}) collective-permute-start(bf16[1,128,512]{2,1,0:T(8,128)(2,1)} %get-tuple-element.6), channel_id=1, source_target_pairs={{1,0},{2,1},{3,2},{4,3},{5,4},{6,5},{7,6},{8,7},{9,8},{10,9},{11,1... | collective-permute-start | bytes 393224 | tf_op jit(solution)/shard_map/ppermute | solution.py:18
  16.5 25.7 %collective-permute-start = (bf16[1,128,512]{2,1,0:T(8,128)(2,1)}, bf16[1,128,512]{2,1,0:T(8,128)(2,1)}, u32[]{:S(2)}, u32[]{:S(2)}) collective-permute-start(bf16[1,128,512]{2,1,0:T(8,128)(2,1)} %get-tuple-element.7), channel_id=1, source_target_pairs={{0,1},{1,2},{2,3},{3,4},{4,5},{5,6},{6,7},{7,8},{8,9},{9,10},{10,1... | collective-permute-start | bytes 393224 | tf_op jit(solution)/shard_map/ppermute | solution.py:15
  23.6 27.3 %copy-start.9 = (pred[32,512]{1,0:T(8,128)(4,1)}, pred[32,512]{1,0:T(8,128)(4,1)S(1)}, u32[]{:S(2)}) copy-start(pred[32,512]{1,0:T(8,128)(4,1)S(1)} %copy.28) | copy-start | bytes 49156
  29.5 21.4 %all-to-all-start.1 = ((bf16[32,2,8,512]{3,2,1,0:T(8,128)(2,1)}), bf16[32,2,8,512]{3,2,1,0:T(8,128)(2,1)}, u32[]{:S(2)}, u32[]{:S(2)}) async-start(bf16[32,2,8,512]{3,2,1,0:T(8,128)(2,1)} %bitcast.85), calls=%async_computation.1 | async-start | bytes 1048576 | tf_op jit(solution)/shard_map/all_to_all | solution.py:25
  35.3 6.8 %copy-start.11 = (s32[4096]{0:T(1024)S(1)}, s32[4096]{0:T(1024)}, u32[]{:S(2)}) copy-start(s32[4096]{0:T(1024)} %param.8) | copy-start | bytes 49156
  35.4 6.8 %copy-start = (bf16[4096,512]{1,0:T(8,128)(2,1)S(1)}, bf16[4096,512]{1,0:T(8,128)(2,1)}, u32[]{:S(2)}) copy-start(bf16[4096,512]{1,0:T(8,128)(2,1)} %param.7) | copy-start | bytes 12582916
  50.9 6.8 %copy-start.1 = (bf16[4096,512]{1,0:T(8,128)(2,1)S(1)}, bf16[4096,512]{1,0:T(8,128)(2,1)}, u32[]{:S(2)}) copy-start(bf16[4096,512]{1,0:T(8,128)(2,1)} %param.7) | copy-start | bytes 12582916
  76.3 2.0 %copy-start.3 = (bf16[32,128,512]{2,1,0:T(8,128)(2,1)}, bf16[32,128,512]{2,1,0:T(8,128)(2,1)S(1)}, u32[]{:S(2)}) copy-start(bf16[32,128,512]{2,1,0:T(8,128)(2,1)S(1)} %fusion.2) | copy-start | bytes 12582916
  79.0 21.4 %collective-permute-start.2 = (bf16[1,128,512]{2,1,0:T(8,128)(2,1)}, bf16[1,128,512]{2,1,0:T(8,128)(2,1)S(1)}, u32[]{:S(2)}, u32[]{:S(2)}) collective-permute-start(bf16[1,128,512]{2,1,0:T(8,128)(2,1)} %get-tuple-element.5), channel_id=1, source_target_pairs={{0,1},{1,2},{2,3},{3,4},{4,5},{5,6},{6,7},{7,8},{8,9},{9,10},{10,1... | collective-permute-start | bytes 393224 | tf_op jit(solution)/shard_map/ppermute | solution.py:15
  82.6 22.3 %all-to-all-start.2 = ((bf16[32,2,8,512]{3,2,1,0:T(8,128)(2,1)}), bf16[32,2,8,512]{3,2,1,0:T(8,128)(2,1)}, u32[]{:S(2)}, u32[]{:S(2)}) async-start(bf16[32,2,8,512]{3,2,1,0:T(8,128)(2,1)} %bitcast.84), calls=%async_computation.2 | async-start | bytes 1048576 | tf_op jit(solution)/shard_map/all_to_all | solution.py:25
  88.4 11.9 %copy-start.4 = (bf16[32,128,512]{2,1,0:T(8,128)(2,1)S(1)}, bf16[32,128,512]{2,1,0:T(8,128)(2,1)}, u32[]{:S(2)}) copy-start(bf16[32,128,512]{2,1,0:T(8,128)(2,1)} %copy-done.3) | copy-start | bytes 12582916
  95.2 9.6 %copy-start.10 = (pred[32,512]{1,0:T(8,128)(4,1)S(1)}, pred[32,512]{1,0:T(8,128)(4,1)}, u32[]{:S(2)}) copy-start(pred[32,512]{1,0:T(8,128)(4,1)} %copy-done.9) | copy-start | bytes 49156
  95.2 16.4 %collective-permute-start.3 = (bf16[1,128,512]{2,1,0:T(8,128)(2,1)}, bf16[1,128,512]{2,1,0:T(8,128)(2,1)}, u32[]{:S(2)}, u32[]{:S(2)}) collective-permute-start(bf16[1,128,512]{2,1,0:T(8,128)(2,1)} %get-tuple-element.4), channel_id=1, source_target_pairs={{1,0},{2,1},{3,2},{4,3},{5,4},{6,5},{7,6},{8,7},{9,8},{10,9},{11,1... | collective-permute-start | bytes 393224 | tf_op jit(solution)/shard_map/ppermute | solution.py:18
  104.8 6.8 %copy-start.5 = (bf16[32,128,512]{2,1,0:T(8,128)(2,1)S(1)}, bf16[32,128,512]{2,1,0:T(8,128)(2,1)}, u32[]{:S(2)}) copy-start(bf16[32,128,512]{2,1,0:T(8,128)(2,1)} %copy-done.3) | copy-start | bytes 12582916
  111.6 13.8 %copy-start.2 = (bf16[4096,512]{1,0:T(8,128)(2,1)S(1)}, bf16[4096,512]{1,0:T(8,128)(2,1)}, u32[]{:S(2)}) copy-start(bf16[4096,512]{1,0:T(8,128)(2,1)} %param.7) | copy-start | bytes 12582916
  130.4 3.1 %copy-start.7 = (bf16[32,128,512]{2,1,0:T(8,128)(2,1)}, bf16[32,128,512]{2,1,0:T(8,128)(2,1)S(1)}, u32[]{:S(2)}) copy-start(bf16[32,128,512]{2,1,0:T(8,128)(2,1)S(1)} %fusion.3) | copy-start | bytes 12582916
where the time goes:
time: 135 us; the launch traced here: 134 us
  matrix products  64.3 us (48%)
  starting transfers between devices  29.4 us (22%)
  other arithmetic  20.4 us (15%)
  local copies, waits for them, and re-layouts  15.7 us (12%)
  waiting for transfers between devices  3.36 us (2%)
    dot_general x6, matrix products, body(): jnp.einsum('itr,irc->itc', band_w[:, offset + 1], source, preferred_eleme...  50.8 us
    dot_general x2, matrix products, body(): jnp.einsum('tqr,qc->trc', placed, received.reshape(-1, classes), preferre...  13.5 us
    all_to_all x2, starting transfers between devices, fetch_blocks(): lax.all_to_all(blocks, 'node', split_axis=0, concat_axis=0, tiled=True)  11.7 us
    ppermute x2, starting transfers between devices, with_halo(): lax.ppermute(lax.slice_in_dim(block, 0, width, axis=dim), axis, backward)  10.2 us
    convert_element_type x2, other arithmetic, body(): fresh = jnp.where(seeded, clamped, scaled).astype(jnp.bfloat16)  9.95 us
    all_to_all x1, starting transfers between devices, body(): lax.all_to_all(far_block, 'node', split_axis=1, concat_axis=0, tiled=True)  7.45 us
    gather x2, local copies, waits for them, and re-layouts, fetch_blocks(): blocks = current.reshape(-1, block_rows, classes)[requests]  7.15 us
    unnamed x26, local copies, waits for them, and re-layouts  4.35 us
  transfers between devices with their start and end apart: 7, of which 1 were waited for; matrix products, arithmetic and copies ran while one was open for 41% of the time, Pallas kernels for 0%

commit v1 on v0

--- a/solution.py
+++ b/solution.py
@@ -37,9 +37,12 @@
     peer_count = far_w.shape[1]
     slot_count = far_w.shape[2]
     block_rows = far_w.shape[3]
-    requests = lax.all_to_all(far_block, "node", split_axis=1, concat_axis=0, tiled=True).reshape(
-        peer_count, slot_count
-    )
+    requests = jnp.concatenate(
+        lax.all_to_all(
+            jnp.stack(jnp.split(far_block, lax.axis_size("node"), axis=1)), "node", 0, 0
+        ),
+        axis=0,
+    ).reshape(peer_count, slot_count)
     live_slots = jnp.arange(slot_count)[None, :] < far_count[0][:, None]
     weights = jnp.where(live_slots[:, :, None, None], far_w[0], jnp.zeros((), jnp.bfloat16))
     flat_tiles = far_tile[0].reshape(-1)

time: 135 us -> 154 us (1.14)
  local copies, waits for them, and re-layouts: 15.7 us -> 35.1 us
    unnamed x26 -> x56, local copies, waits for them, and re-layouts: 4.35 us -> 19.7 us
    split x0 -> x2, local copies, waits for them, and re-layouts: none -> 3.46 us  [body(): jnp.split(far_block, lax.axis_size('node'), axis=1)]
  transfers between devices with their start and end apart: 7 -> 7, of which waited for: 1 -> 1; matrix products, arithmetic and copies ran while one was open for 41% -> 36% of each run, Pallas kernels for 0% -> 0%
where the time goes in v1:
time: 154 us; the launch traced here: 153 us
  matrix products  64.2 us (42%)
  local copies, waits for them, and re-layouts  35.1 us (23%)
  starting transfers between devices  29.4 us (19%)
  other arithmetic  20.4 us (13%)
  waiting for transfers between devices  3.38 us (2%)
    dot_general x6, matrix products, body(): jnp.einsum('itr,irc->itc', band_w[:, offset + 1], source, preferred_eleme...  50.7 us
    unnamed x56, local copies, waits for them, and re-layouts  19.7 us
    dot_general x2, matrix products, body(): jnp.einsum('tqr,qc->trc', placed, received.reshape(-1, classes), preferre...  13.5 us
    all_to_all x2, starting transfers between devices, fetch_blocks(): lax.all_to_all(blocks, 'node', split_axis=0, concat_axis=0, tiled=True)  11.7 us
    ppermute x2, starting transfers between devices, with_halo(): lax.ppermute(lax.slice_in_dim(block, 0, width, axis=dim), axis, backward)  10.2 us
    convert_element_type x2, other arithmetic, body(): fresh = jnp.where(seeded, clamped, scaled).astype(jnp.bfloat16)  9.95 us
    all_to_all x1, starting transfers between devices, body(): lax.all_to_all(jnp.stack(jnp.split(far_block, lax.axis_size('node'), axis...  7.45 us
    gather x2, local copies, waits for them, and re-layouts, fetch_blocks(): blocks = current.reshape(-1, block_rows, classes)[requests]  7.15 us
  transfers between devices with their start and end apart: 7, of which 1 were waited for; matrix products, arithmetic and copies ran while one was open for 36% of the time, Pallas kernels for 0%

profile of v1, /device:TPU:0, one launch (start us, length us, event | category | flops | bytes accessed | tf_op | source)
XLA Modules:
  0.0 153.4 jit_solution(6529493488995585212)
XLA Ops:
  0.7 1.6 %slice_reduce_fusion.1 = (s32[2]{0:T(128)S(1)}, s32[2]{0:T(128)S(1)}, s32[2]{0:T(128)S(1)}, s32[2]{0:T(128)S(1)}, s32[2]{0:T(128)S(1)}, /*index=5*/s32[2]{0:T(12...) fusion(s32[1,32,2]{1,2,0:T(2,128)} %param.10), kind=kLoop, calls=%fused_computation.104 | loop fusion | bytes 208 | tf_op jit(solution)/shard_map/split | solution.py:42
  2.2 1.9 %slice_reduce_fusion = (s32[2]{0:T(128)S(1)}, s32[2]{0:T(128)S(1)}, s32[2]{0:T(128)S(1)}, s32[2]{0:T(128)S(1)}, s32[2]{0:T(128)S(1)}, /*index=5*/s32[2]{0:T(128)...) fusion(s32[1,32,2]{1,2,0:T(2,128)} %param.10), kind=kLoop, calls=%fused_computation.103 | loop fusion | bytes 304 | tf_op jit(solution)/shard_map/split | solution.py:42
  12.8 0.6 constant_dynamic-update-slice_fusion.15
  21.6 7.5 %all-to-all-start = ((s32[32,1,1,2]{3,2,1,0:T(1,128)}), s32[32,1,1,2]{3,2,1,0:T(1,128)}, u32[]{:S(2)}, u32[]{:S(2)}) async-start(s32[32,1,1,2]{3,2,1,0:T(1,128)} %constant_dynamic-update-slice_fusion), calls=%async_computation | async-start | bytes 32768 | tf_op jit(solution)/shard_map/all_to_all | solution.py:41
  29.1 1.7 %slice_bitcast_fusion = (bf16[1,128,512]{2,1,0:T(8,128)(2,1)}, bf16[1,128,512]{2,1,0:T(8,128)(2,1)}) fusion(bf16[4096,512]{1,0:T(8,128)(2,1)} %param.7), kind=kLoop, calls=%fused_computation.59 | loop fusion | bytes 524288 | tf_op jit(solution)/shard_map/slice | solution.py:18
  30.8 5.1 %collective-permute-start.1 = (bf16[1,128,512]{2,1,0:T(8,128)(2,1)}, bf16[1,128,512]{2,1,0:T(8,128)(2,1)}, u32[]{:S(2)}, u32[]{:S(2)}) collective-permute-start(bf16[1,128,512]{2,1,0:T(8,128)(2,1)} %get-tuple-element.38), channel_id=1, source_target_pairs={{1,0},{2,1},{3,2},{4,3},{5,4},{6,5},{7,6},{8,7},{9,8},{10,9},{11,1... | collective-permute-start | bytes 393224 | tf_op jit(solution)/shard_map/ppermute | solution.py:18
  35.9 0.8 copy.111
  36.9 0.7 iota_compare_fusion.1
  38.5 2.5 %convert_reduce_fusion = f32[32,128]{1,0:T(8,128)S(1)} fusion(bf16[32,3,128,128]{3,2,1,0:T(8,128)(2,1)} %param.9), kind=kLoop, calls=%fused_computation.19 | loop fusion | flops 3141632 | bytes 3162112 | tf_op jit(solution)/shard_map/reduce_sum | solution.py:51
  41.1 1.0 bitcast_select_fusion.1
  42.1 0.8 convert_reduce_fusion.1
  43.2 1.1 scatter_fusion
  44.3 0.8 copy.114
  45.3 3.6 %gather_fusion = bf16[64,8,512]{2,1,0:T(8,128)(2,1)} fusion(bf16[512,8,512]{2,1,0:T(8,128)(2,1)} %bitcast.141, s32[1024]{0:T(1024)S(1)} %pad_clamp_fusion), kind=kCustom, calls=%fused_computation | custom fusion | bytes 1048832 | tf_op jit(solution)/shard_map/gather | solution.py:24
  48.9 5.8 %all-to-all-start.1 = ((bf16[32,2,8,512]{3,2,1,0:T(8,128)(2,1)}), bf16[32,2,8,512]{3,2,1,0:T(8,128)(2,1)}, u32[]{:S(2)}, u32[]{:S(2)}) async-start(bf16[32,2,8,512]{3,2,1,0:T(8,128)(2,1)} %bitcast.149), calls=%async_computation.1 | async-start | bytes 1048576 | tf_op jit(solution)/shard_map/all_to_all | solution.py:25
  54.8 6.8 %fusion.29 = f32[32,128,512]{2,1,0:T(8,128)} fusion(bf16[32,128,512]{2,1,0:T(8,128)(2,1)} %bitcast.142, bf16[32,3,128,128]{3,2,1,0:T(8,128)(2,1)S(1)} %copy-done.6), kind=kOutput, calls=%fused_computation.46 | convolution fusion | flops 536870912 | bytes 13631488 | tf_op jit(solution)/shard_map/itr,irc->itc/dot_general | solution.py:66
  61.6 5.4 %fusion.17 = f32[32,512,128]{1,2,0:T(8,128)} fusion(bf16[32,128,512]{2,1,0:T(8,128)(2,1)S(1)} %bitcast.143, bf16[1,128,512]{2,1,0:T(8,128)(2,1)} %collective-permute-done, bf16[32,3,128,128]{3,2,1,0:T(8,128)(2,1)S(1)} %copy-done.6), kind=kOutput, calls=%fused_computation.34 | convolution fusion | flops 545259520 | bytes 13762560 | tf_op jit(solution)/shard_map/itr,irc->itc/dot_general | solution.py:66
  67.0 3.4 %all-to-all-done.1 = bf16[32,2,8,512]{3,2,1,0:T(8,128)(2,1)} async-done(((bf16[32,2,8,512]{3,2,1,0:T(8,128)(2,1)}), bf16[32,2,8,512]{3,2,1,0:T(8,128)(2,1)}, u32[]{:S(2)}, u32[]{:S(2)}) %all-to-all-start.1) | async-done | bytes 524320 | tf_op jit(solution)/shard_map/all_to_all | solution.py:25
  70.4 6.8 %fusion.9 = f32[32,128,512]{2,1,0:T(8,128)} fusion(bf16[512,512,1]{1,0,2:T(8,128)(2,1)} %bitcast.16, pred[32,512]{1,0:T(8,128)(4,1)S(1)} %copy.112, bf16[512,128]{0,1:T(8,128)(2,1)S(1)} %copy.113), kind=kOutput, calls=%fused_computation.22 | convolution fusion | flops 2149580800 | bytes 9060352 | tf_op jit(solution)/shard_map/tqr,qc->trc/dot_general | solution.py:69
  77.1 13.6 %multiply_reduce_fusion.1 = (f32[32,128]{1,0:T(8,128)S(1)}, f32[32,128,512]{2,1,0:T(8,128)}) fusion(f32[32,128]{1,0:T(8,128)S(1)} %scatter_fusion, f32[32,128,512]{2,1,0:T(8,128)} %fusion.9, bf16[1,128,512]{2,1,0:T(8,128)(2,1)} %collective-permute-done.1, bf16[32,128,512]{2,1,0:T(8,128)(2,1)S(1)} %bitcast.144, bf16[32,3,128,128]{3,2,1,0:T(8,128)(2,1)S(1)} %copy-done.6, ...), kind=kOutput, calls=%fused_computation.18 | convolution fusion | flops 557838336 | bytes 38961152 | tf_op jit(solution)/shard_map/itr,irc->itc/dot_general | solution.py:66
  90.7 5.0 %fusion.2 = bf16[32,128,512]{2,1,0:T(8,128)(2,1)S(1)} fusion(f32[32,128,512]{2,1,0:T(8,128)} %get-tuple-element.41, f32[32,128]{1,0:T(8,128)S(1)} %maximum_multiply_fusion.1, pred[32,128]{1,0:T(8,128)(4,1)S(1)} %compare_bitcast_fusion, bf16[4096,512]{1,0:T(8,128)(2,1)S(1)} %copy-done.1), kind=kLoop, calls=%fused_computation.9 | loop fusion | flops 8388608 | bytes 16797696 | tf_op jit(solution)/shard_map/convert_element_type | solution.py:75
  95.7 2.0 %copy-done.3 = bf16[32,128,512]{2,1,0:T(8,128)(2,1)} copy-done((bf16[32,128,512]{2,1,0:T(8,128)(2,1)}, bf16[32,128,512]{2,1,0:T(8,128)(2,1)S(1)}, u32[]{:S(2)}) %copy-start.3) | copy-done | bytes 4194328
  97.7 0.7 fusion.46
  98.4 3.6 %gather_fusion.1 = bf16[64,8,512]{2,1,0:T(8,128)(2,1)} fusion(bf16[512,8,512]{2,1,0:T(8,128)(2,1)} %bitcast.146, s32[1024]{0:T(1024)S(1)} %pad_clamp_fusion), kind=kCustom, calls=%fused_computation.1 | custom fusion | bytes 1048832 | tf_op jit(solution)/shard_map/gather | solution.py:24
  102.0 5.8 %all-to-all-start.2 = ((bf16[32,2,8,512]{3,2,1,0:T(8,128)(2,1)}), bf16[32,2,8,512]{3,2,1,0:T(8,128)(2,1)}, u32[]{:S(2)}, u32[]{:S(2)}) async-start(bf16[32,2,8,512]{3,2,1,0:T(8,128)(2,1)} %bitcast.148), calls=%async_computation.2 | async-start | bytes 1048576 | tf_op jit(solution)/shard_map/all_to_all | solution.py:25
  107.9 6.8 %fusion.27 = f32[32,512,128]{1,2,0:T(8,128)} fusion(bf16[32,128,512]{2,1,0:T(8,128)(2,1)} %copy-done.3, bf16[32,3,128,128]{3,2,1,0:T(8,128)(2,1)S(1)} %copy-done.6), kind=kOutput, calls=%fused_computation.44 | convolution fusion | flops 536870912 | bytes 13631488 | tf_op jit(solution)/shard_map/itr,irc->itc/dot_general | solution.py:66
  114.7 5.1 %collective-permute-start.3 = (bf16[1,128,512]{2,1,0:T(8,128)(2,1)}, bf16[1,128,512]{2,1,0:T(8,128)(2,1)}, u32[]{:S(2)}, u32[]{:S(2)}) collective-permute-start(bf16[1,128,512]{2,1,0:T(8,128)(2,1)} %get-tuple-element.36), channel_id=1, source_target_pairs={{1,0},{2,1},{3,2},{4,3},{5,4},{6,5},{7,6},{8,7},{9,8},{10,9},{11,1... | collective-permute-start | bytes 393224 | tf_op jit(solution)/shard_map/ppermute | solution.py:18
  119.8 4.5 %fusion.13 = f32[32,512,128]{1,2,0:T(8,128)} fusion(bf16[32,128,512]{2,1,0:T(8,128)(2,1)S(1)} %copy-done.4, bf16[1,128,512]{2,1,0:T(8,128)(2,1)S(1)} %collective-permute-done.2, bf16[32,3,128,128]{3,2,1,0:T(8,128)(2,1)S(1)} %copy-done.6), kind=kOutput, calls=%fused_computation.28 | convolution fusion | flops 545259520 | bytes 13762560 | tf_op jit(solution)/shard_map/itr,irc->itc/dot_general | solution.py:66
  124.3 6.8 %fusion.7 = f32[32,128,512]{2,1,0:T(8,128)} fusion(bf16[512,512,1]{1,0,2:T(8,128)(2,1)} %bitcast.24, pred[32,512]{1,0:T(8,128)(4,1)S(1)} %copy-done.10, bf16[512,128]{0,1:T(8,128)(2,1)S(1)} %copy.113), kind=kOutput, calls=%fused_computation.20 | convolution fusion | flops 2149580800 | bytes 9060352 | tf_op jit(solution)/shard_map/tqr,qc->trc/dot_general | solution.py:69
  131.0 13.7 %multiply_reduce_fusion = (f32[32,128]{1,0:T(8,128)S(1)}, f32[32,128,512]{2,1,0:T(8,128)}) fusion(f32[32,128]{1,0:T(8,128)S(1)} %scatter_fusion, f32[32,128,512]{2,1,0:T(8,128)} %fusion.7, bf16[1,128,512]{2,1,0:T(8,128)(2,1)} %collective-permute-done.3, bf16[32,128,512]{2,1,0:T(8,128)(2,1)S(1)} %copy-done.5, bf16[32,3,128,128]{3,2,1,0:T(8,128)(2,1)} %param.9, ...), kind=kOutput, calls=%fused_computation.17 | convolution fusion | flops 557838336 | bytes 38961152 | tf_op jit(solution)/shard_map/itr,irc->itc/dot_general | solution.py:66
  144.8 5.0 %fusion.3 = bf16[32,128,512]{2,1,0:T(8,128)(2,1)S(1)} fusion(f32[32,128,512]{2,1,0:T(8,128)} %get-tuple-element.43, f32[32,128]{1,0:T(8,128)S(1)} %maximum_multiply_fusion, pred[32,128]{1,0:T(8,128)(4,1)S(1)} %compare_bitcast_fusion, bf16[4096,512]{1,0:T(8,128)(2,1)S(1)} %copy-done.2), kind=kLoop, calls=%fused_computation.10 | loop fusion | flops 8388608 | bytes 16797696 | tf_op jit(solution)/shard_map/convert_element_type | solution.py:75
  149.8 3.1 %fusion.5 = (f32[32]{0:T(128)S(1)}, f32[32]{0:T(128)S(1)}) fusion(bf16[32,128,512]{2,1,0:T(8,128)(2,1)S(1)} %bitcast.145, bf16[32,128,512]{2,1,0:T(8,128)(2,1)S(1)} %copy-done.5, bf16[32,128,512]{2,1,0:T(8,128)(2,1)S(1)} %fusion.3), kind=kLoop, calls=%fused_computation.12 | loop fusion | flops 18874304 | bytes 12583168 | tf_op jit(solution)/shard_map/reduce_sum | solution.py:77
  (80 shorter events, 19.1 us)
Async XLA Ops:
  0.6 54.1 %copy-start.6 = (bf16[32,3,128,128]{3,2,1,0:T(8,128)(2,1)S(1)}, bf16[32,3,128,128]{3,2,1,0:T(8,128)(2,1)}, u32[]{:S(2)}) copy-start(bf16[32,3,128,128]{3,2,1,0:T(8,128)(2,1)} %param.9) | copy-start | bytes 9437188
  0.6 41.5 %copy-start.8 = (bf16[1,32,2,8,128]{4,3,2,1,0:T(8,128)(2,1)S(1)}, bf16[1,32,2,8,128]{4,3,2,1,0:T(8,128)(2,1)}, u32[]{:S(2)}) copy-start(bf16[1,32,2,8,128]{4,3,2,1,0:T(8,128)(2,1)} %param.13) | copy-start | bytes 393220
  21.6 22.7 %all-to-all-start = ((s32[32,1,1,2]{3,2,1,0:T(1,128)}), s32[32,1,1,2]{3,2,1,0:T(1,128)}, u32[]{:S(2)}, u32[]{:S(2)}) async-start(s32[32,1,1,2]{3,2,1,0:T(1,128)} %constant_dynamic-update-slice_fusion), calls=%async_computation | async-start | bytes 32768 | tf_op jit(solution)/shard_map/all_to_all | solution.py:41
  30.8 46.3 %collective-permute-start.1 = (bf16[1,128,512]{2,1,0:T(8,128)(2,1)}, bf16[1,128,512]{2,1,0:T(8,128)(2,1)}, u32[]{:S(2)}, u32[]{:S(2)}) collective-permute-start(bf16[1,128,512]{2,1,0:T(8,128)(2,1)} %get-tuple-element.38), channel_id=1, source_target_pairs={{1,0},{2,1},{3,2},{4,3},{5,4},{6,5},{7,6},{8,7},{9,8},{10,9},{11,1... | collective-permute-start | bytes 393224 | tf_op jit(solution)/shard_map/ppermute | solution.py:18
  35.9 25.7 %collective-permute-start = (bf16[1,128,512]{2,1,0:T(8,128)(2,1)}, bf16[1,128,512]{2,1,0:T(8,128)(2,1)}, u32[]{:S(2)}, u32[]{:S(2)}) collective-permute-start(bf16[1,128,512]{2,1,0:T(8,128)(2,1)} %get-tuple-element.39), channel_id=1, source_target_pairs={{0,1},{1,2},{2,3},{3,4},{4,5},{5,6},{6,7},{7,8},{8,9},{9,10},{10,1... | collective-permute-start | bytes 393224 | tf_op jit(solution)/shard_map/ppermute | solution.py:15
  43.0 27.3 %copy-start.9 = (pred[32,512]{1,0:T(8,128)(4,1)}, pred[32,512]{1,0:T(8,128)(4,1)S(1)}, u32[]{:S(2)}) copy-start(pred[32,512]{1,0:T(8,128)(4,1)S(1)} %copy.112) | copy-start | bytes 49156
  48.9 21.4 %all-to-all-start.1 = ((bf16[32,2,8,512]{3,2,1,0:T(8,128)(2,1)}), bf16[32,2,8,512]{3,2,1,0:T(8,128)(2,1)}, u32[]{:S(2)}, u32[]{:S(2)}) async-start(bf16[32,2,8,512]{3,2,1,0:T(8,128)(2,1)} %bitcast.149), calls=%async_computation.1 | async-start | bytes 1048576 | tf_op jit(solution)/shard_map/all_to_all | solution.py:25
  54.8 6.8 %copy-start.11 = (s32[4096]{0:T(1024)S(1)}, s32[4096]{0:T(1024)}, u32[]{:S(2)}) copy-start(s32[4096]{0:T(1024)} %param.8) | copy-start | bytes 49156
  54.8 6.8 %copy-start = (bf16[4096,512]{1,0:T(8,128)(2,1)S(1)}, bf16[4096,512]{1,0:T(8,128)(2,1)}, u32[]{:S(2)}) copy-start(bf16[4096,512]{1,0:T(8,128)(2,1)} %param.7) | copy-start | bytes 12582916
  70.4 6.8 %copy-start.1 = (bf16[4096,512]{1,0:T(8,128)(2,1)S(1)}, bf16[4096,512]{1,0:T(8,128)(2,1)}, u32[]{:S(2)}) copy-start(bf16[4096,512]{1,0:T(8,128)(2,1)} %param.7) | copy-start | bytes 12582916
  95.7 2.0 %copy-start.3 = (bf16[32,128,512]{2,1,0:T(8,128)(2,1)}, bf16[32,128,512]{2,1,0:T(8,128)(2,1)S(1)}, u32[]{:S(2)}) copy-start(bf16[32,128,512]{2,1,0:T(8,128)(2,1)S(1)} %fusion.2) | copy-start | bytes 12582916
  98.4 21.4 %collective-permute-start.2 = (bf16[1,128,512]{2,1,0:T(8,128)(2,1)}, bf16[1,128,512]{2,1,0:T(8,128)(2,1)S(1)}, u32[]{:S(2)}, u32[]{:S(2)}) collective-permute-start(bf16[1,128,512]{2,1,0:T(8,128)(2,1)} %get-tuple-element.37), channel_id=1, source_target_pairs={{0,1},{1,2},{2,3},{3,4},{4,5},{5,6},{6,7},{7,8},{8,9},{9,10},{10,1... | collective-permute-start | bytes 393224 | tf_op jit(solution)/shard_map/ppermute | solution.py:15
  102.0 22.2 %all-to-all-start.2 = ((bf16[32,2,8,512]{3,2,1,0:T(8,128)(2,1)}), bf16[32,2,8,512]{3,2,1,0:T(8,128)(2,1)}, u32[]{:S(2)}, u32[]{:S(2)}) async-start(bf16[32,2,8,512]{3,2,1,0:T(8,128)(2,1)} %bitcast.148), calls=%async_computation.2 | async-start | bytes 1048576 | tf_op jit(solution)/shard_map/all_to_all | solution.py:25
  107.8 11.9 %copy-start.4 = (bf16[32,128,512]{2,1,0:T(8,128)(2,1)S(1)}, bf16[32,128,512]{2,1,0:T(8,128)(2,1)}, u32[]{:S(2)}) copy-start(bf16[32,128,512]{2,1,0:T(8,128)(2,1)} %copy-done.3) | copy-start | bytes 12582916
  114.7 9.6 %copy-start.10 = (pred[32,512]{1,0:T(8,128)(4,1)S(1)}, pred[32,512]{1,0:T(8,128)(4,1)}, u32[]{:S(2)}) copy-start(pred[32,512]{1,0:T(8,128)(4,1)} %copy-done.9) | copy-start | bytes 49156
  114.7 16.4 %collective-permute-start.3 = (bf16[1,128,512]{2,1,0:T(8,128)(2,1)}, bf16[1,128,512]{2,1,0:T(8,128)(2,1)}, u32[]{:S(2)}, u32[]{:S(2)}) collective-permute-start(bf16[1,128,512]{2,1,0:T(8,128)(2,1)} %get-tuple-element.36), channel_id=1, source_target_pairs={{1,0},{2,1},{3,2},{4,3},{5,4},{6,5},{7,6},{8,7},{9,8},{10,9},{11,1... | collective-permute-start | bytes 393224 | tf_op jit(solution)/shard_map/ppermute | solution.py:18
  124.3 6.8 %copy-start.5 = (bf16[32,128,512]{2,1,0:T(8,128)(2,1)S(1)}, bf16[32,128,512]{2,1,0:T(8,128)(2,1)}, u32[]{:S(2)}) copy-start(bf16[32,128,512]{2,1,0:T(8,128)(2,1)} %copy-done.3) | copy-start | bytes 12582916
  131.0 13.7 %copy-start.2 = (bf16[4096,512]{1,0:T(8,128)(2,1)S(1)}, bf16[4096,512]{1,0:T(8,128)(2,1)}, u32[]{:S(2)}) copy-start(bf16[4096,512]{1,0:T(8,128)(2,1)} %param.7) | copy-start | bytes 12582916
  149.7 3.1 %copy-start.7 = (bf16[32,128,512]{2,1,0:T(8,128)(2,1)}, bf16[32,128,512]{2,1,0:T(8,128)(2,1)S(1)}, u32[]{:S(2)}) copy-start(bf16[32,128,512]{2,1,0:T(8,128)(2,1)S(1)} %fusion.3) | copy-start | bytes 12582916
